TPU v7x, 128 devices: a whole 4x4x4 slice. The times are simulated.
128 devices in a mesh: row: 32 (over z, x, core), col: 4 (over y).
Axes of the slice: x: 4, y: 4, z: 4, core: 2. Of those that a mesh axis runs over, the one named last changes fastest.
Arguments:
- spikes: int32 [10, 16384], P(None, ('row', 'col')), may hold values 0 or 1
- stp_init: float32 [2, 16384], P(None, ('row', 'col')), may hold values from 0.2 to 1
- trace_init: float32 [3, 16384], P(None, ('row', 'col')), may hold values from 0 to 1.5
- weights: float32 [32, 4, 256, 128, 128], P('row', 'col'), may hold values from 0 to 1
- block_pre: int32 [32, 4, 256], P('row', 'col'), may hold values from 0 to 31
- block_post: int32 [32, 4, 256], P('row', 'col'), may hold values from 0 to 3
- block_count: int32 [32, 4], P('row', 'col'), may hold values from 1 to 255, as said below
Outputs:
- new_weights: float32 [32, 4, 128, 128, 128], P('row', 'col')
- synaptic: float32 [10, 16384], P(None, ('row', 'col'))
Inputs may be any that keep to these rules, and one draw needn't show every extreme that they name: block_count[r, c] + block_count[(r + 16) mod 32, c] = 256; some device uses 2 * 128 - 1 slots in every draw.
All inputs are finite; a program needn't handle non-finite values. No bound on the sum of `spikes` on one device may be relied on, other than what follows from the above.
Results may differ from a plain program's by a relative error of at most 0.0003.
Values sent between devices are 32-bit elements; how exact they have to be, the bound alone decides.
A program may use at most 128 MiB of HBM per device.

v0:
```python
import math

import jax
import jax.numpy as jnp
from jax import lax
from jax.sharding import PartitionSpec as P

HIGHEST = lax.Precision.HIGHEST
BASE_USE = 0.25
USE_DECAY = 0.98
SUPPLY_RATE = 0.005
PLUS_DECAY = math.exp(-1.0 / 16.8)
MINUS_DECAY = math.exp(-1.0 / 33.7)
SLOW_DECAY = math.exp(-1.0 / 114.0)
SYN_DECAY = math.exp(-1.0 / 5.0)
PAIR_UP = 1.0
TRIPLET_UP = 0.8
PAIR_DOWN = 0.9
LEARN_RATE = 0.02
WEIGHT_MAX = 1.0
INHIB_GAIN = 4.0


def in_order(tiles, dim):
    lengths = list(tiles.shape[1:])
    lengths[dim] *= tiles.shape[0]
    return jnp.moveaxis(tiles, 0, dim).reshape(lengths)


def copy_for_each(shard, axis):
    size = lax.axis_size(axis)
    return lax.all_to_all(
        jnp.broadcast_to(shard[None], (size, *shard.shape)), axis, 0, 0, tiled=True
    )


def collect(shard, axis, dim):
    return in_order(copy_for_each(shard, axis), dim)


def from_partner(value, axis, distance):
    mask = 2**distance
    pairs = [(source, source ^ mask) for source in range(lax.axis_size(axis))]
    return lax.ppermute(value, axis, pairs)


def cut_along(shard, dim, size):
    before, after = (shard.shape[:dim], shard.shape[dim + 1 :])
    return jnp.moveaxis(shard.reshape(*before, size, -1, *after), dim, 0)


def sum_at_owner(shard, axis, dim):
    tiles = cut_along(shard, dim, lax.axis_size(axis))
    arrived = lax.all_to_all(tiles, axis, split_axis=0, concat_axis=0, tiled=True)
    return arrived.sum(axis=0)


def neuron_traces(spikes, stp_init, trace_init):
    fired = spikes.astype(jnp.float32)

    def neuron_advance(carry, fired_now):
        use_level, supply, pre_fast, post_fast, post_slow = carry
        use_level = BASE_USE + (use_level - BASE_USE) * USE_DECAY
        use_level = use_level + fired_now * BASE_USE * (1.0 - use_level)
        release = fired_now * use_level * supply
        supply = supply + SUPPLY_RATE * (1.0 - supply) - release
        pre_fast = pre_fast * PLUS_DECAY + fired_now
        potent = fired_now * (PAIR_UP + TRIPLET_UP * post_slow)
        depress = PAIR_DOWN * post_fast
        post_fast = post_fast * MINUS_DECAY + fired_now
        post_slow = post_slow * SLOW_DECAY + fired_now
        return (
            (use_level, supply, pre_fast, post_fast, post_slow),
            (release, pre_fast, potent, depress),
        )

    start = (stp_init[0], stp_init[1], trace_init[0], trace_init[1], trace_init[2])
    _, results = lax.scan(neuron_advance, start, fired)
    return results


def block_work(weights, pre_blocks, post_blocks, polarity):
    release = pre_blocks[:, 0]
    pre_fast = pre_blocks[:, 1]
    potent = post_blocks[:, 0]
    depress = post_blocks[:, 1]
    driven = release * polarity
    current = jnp.einsum("nij,nsj->nsi", weights, driven, precision=HIGHEST)
    post_terms = jnp.concatenate([potent, -depress], axis=1)
    pre_terms = jnp.concatenate([pre_fast, release], axis=1)
    change = jnp.einsum("nki,nkj->nij", post_terms, pre_terms, precision=HIGHEST)
    return (current, jnp.clip(weights + LEARN_RATE * change, 0.0, WEIGHT_MAX))


def filtered(drive, gain):

    def filtered_advance(state, current):
        state = state * SYN_DECAY + gain * current
        return (state, state)

    _, result = lax.scan(filtered_advance, jnp.zeros_like(drive[0]), drive)
    return result


def group_sums(current, targets, groups):
    onehot = (targets[:, None] == jnp.arange(groups, dtype=jnp.int32)[None, :]).astype(jnp.float32)
    return jnp.einsum("nq,nsi->qsi", onehot, current, precision=HIGHEST)


def body(spikes, stp_init, trace_init, weights, block_pre, block_post, block_count):
    group = weights.shape[-1]
    slot_total = weights.shape[2]
    half_slots = slot_total // 2
    row_total = lax.axis_size("row")
    col_total = lax.axis_size("col")
    partner_bit = row_total.bit_length() - 2
    polarity = jnp.where(jnp.arange(group) % 5 == 4, -INHIB_GAIN, 1.0).astype(jnp.float32)
    release, pre_fast, potent, depress = neuron_traces(spikes, stp_init, trace_init)
    pre_local = jnp.stack([release, pre_fast])[None]
    post_local = jnp.stack([potent, depress])[None]
    pre_table = collect(pre_local, "row", 0)
    post_table = collect(post_local, "col", 0)
    filled = block_count[0, 0]
    own_weights = weights[0, 0]
    pre_ids = block_pre[0, 0]
    post_ids = block_post[0, 0]
    incoming_weights, incoming_pre, incoming_post = from_partner(
        (own_weights[half_slots:], pre_ids[half_slots:], post_ids[half_slots:]), "row", partner_bit
    )
    places = jnp.arange(half_slots, dtype=jnp.int32)
    keeping = places < filled
    picked = jnp.clip(places - filled, 0, half_slots - 1)
    slot_weights = jnp.where(
        keeping[:, None, None], own_weights[:half_slots], jnp.take(incoming_weights, picked, axis=0)
    )
    slot_pre = jnp.where(keeping, pre_ids[:half_slots], jnp.take(incoming_pre, picked))
    slot_post = jnp.where(
        keeping, post_ids[:half_slots], jnp.take(incoming_post, picked) + col_total
    )
    partner_table = from_partner(post_table, "row", partner_bit)
    both_tables = jnp.concatenate([post_table, partner_table], axis=0)
    current, new_blocks = block_work(
        slot_weights,
        jnp.take(pre_table, slot_pre, axis=0),
        jnp.take(both_tables, slot_post, axis=0),
        polarity,
    )
    combined = group_sums(current, slot_post, 2 * col_total)
    returned = from_partner(combined[col_total:], "row", partner_bit)
    partial_value = combined[:col_total] + returned
    drive = sum_at_owner(partial_value, "col", 0)[0]
    synaptic = filtered(drive, 1.0 / math.sqrt(group * half_slots))
    return (new_blocks[None, None], synaptic)


def solution(mesh):
    placed = (
        P(None, ("row", "col")),
        P(None, ("row", "col")),
        P(None, ("row", "col")),
        P("row", "col", None, None, None),
        P("row", "col", None),
        P("row", "col", None),
        P("row", "col"),
    )
    return jax.shard_map(
        body,
        mesh=mesh,
        in_specs=placed,
        out_specs=(P("row", "col", None, None, None), P(None, ("row", "col"))),
        check_vma=False,
    )
```

profile of v0, /device:TPU:0, one launch (start us, length us, event | category | flops | bytes accessed | tf_op | source)
XLA Modules:
  0.0 275.4 jit_solution(17347714295821259240)
XLA Ops:
  0.6 0.7 slice_bitcast_fusion.4
  1.3 0.0 copy-start.5
  1.3 0.0 copy-start.1
  1.3 0.0 copy-start.3
  1.3 0.0 copy-start.4
  1.3 0.0 copy-start.6
  1.3 4.1 %collective-permute-start.3 = (s32[128]{0:T(128)S(1)}, s32[128]{0:T(128)S(1)}, u32[]{:S(2)}, u32[]{:S(2)}) collective-permute-start(s32[128]{0:T(128)S(1)} %slice_bitcast_fusion.4), channel_id=1, source_target_pairs={{0,64},{4,68},{8,72},{12,76},{16,80},{20,84},{24,88},{28,92},{32,9... | collective-permute-start | bytes 1544 | tf_op jit(solution)/shard_map/ppermute | solution.py:44
  5.4 7.9 %slice_bitcast_fusion = f32[128,128,128]{2,1,0:T(8,128)} fusion(f32[1,1,256,128,128]{4,3,2,1,0:T(8,128)} %param.16), kind=kLoop, calls=%fused_computation.24 | loop fusion | bytes 16777216 | tf_op jit(solution)/shard_map/slice | solution.py:128
  13.3 0.0 collective-permute-start
  13.3 0.0 copy-done.5
  13.3 3.5 %collective-permute-start.1 = (s32[128]{0:T(128)S(1)}, s32[128]{0:T(128)S(1)}, u32[]{:S(2)}, u32[]{:S(2)}) collective-permute-start(s32[128]{0:T(128)S(1)} %slice_bitcast_fusion.10), channel_id=1, source_target_pairs={{0,64},{4,68},{8,72},{12,76},{16,80},{20,84},{24,88},{28,92},{32,9... | collective-permute-start | bytes 1544 | tf_op jit(solution)/shard_map/ppermute | solution.py:44
  16.8 0.0 copy-done.1
  16.8 0.0 copy-done.3
  16.8 0.0 copy-done.4
  16.9 2.2 while.41
  19.1 0.6 broadcast_in_dim.106
  19.7 4.5 %all-to-all-start = ((f32[4,1,2,10,128]{4,2,3,1,0:T(2,128)}), f32[4,1,2,10,128]{4,2,3,1,0:T(2,128)S(1)}, u32[]{:S(2)}, u32[]{:S(2)}) async-start(f32[4,1,2,10,128]{4,2,3,1,0:T(2,128)} %broadcast_in_dim.106), calls=%async_computation | async-start | bytes 81920 | tf_op jit(solution)/shard_map/all_to_all | solution.py:32
  25.0 0.0 collective-permute-done.3
  25.0 1.2 gather_fusion.4
  26.2 170.8 %collective-permute-done.1 = s32[128]{0:T(128)S(1)} collective-permute-done((s32[128]{0:T(128)S(1)}, s32[128]{0:T(128)S(1)}, u32[]{:S(2)}, u32[]{:S(2)}) %collective-permute-start.1) | collective-permute-done | bytes 544 | tf_op jit(solution)/shard_map/ppermute | solution.py:44
  197.0 1.2 gather_fusion.3
  198.3 0.0 copy-done.6
  198.3 0.0 all-to-all-done
  198.3 0.8 broadcast_in_dim.110
  199.1 5.1 %all-to-all-start.1 = ((f32[32,1,2,10,128]{4,2,3,1,0:T(2,128)}), f32[32,1,2,10,128]{4,2,3,1,0:T(2,128)S(1)}, u32[]{:S(2)}, u32[]{:S(2)}) async-start(f32[32,1,2,10,128]{4,2,3,1,0:T(2,128)} %broadcast_in_dim.110), calls=%async_computation.1 | async-start | bytes 655360 | tf_op jit(solution)/shard_map/all_to_all | solution.py:32
  204.3 3.4 %collective-permute-start.2 = (f32[4,2,10,128]{3,1,2,0:T(2,128)S(1)}, f32[4,2,10,128]{3,1,2,0:T(2,128)S(1)}, u32[]{:S(2)}, u32[]{:S(2)}) collective-permute-start(f32[4,2,10,128]{3,1,2,0:T(2,128)S(1)} %bitcast.106), channel_id=1, source_target_pairs={{0,64},{4,68},{8,72},{12,76},{16,80},{20,84},{24,88},{28,92},{32,9... | collective-permute-start | bytes 122888 | tf_op jit(solution)/shard_map/ppermute | solution.py:44
  207.7 3.4 %collective-permute-done.2 = f32[4,2,10,128]{3,1,2,0:T(2,128)S(1)} collective-permute-done((f32[4,2,10,128]{3,1,2,0:T(2,128)S(1)}, f32[4,2,10,128]{3,1,2,0:T(2,128)S(1)}, u32[]{:S(2)}, u32[]{:S(2)}) %collective-permute-start.2) | collective-permute-done | bytes 40992 | tf_op jit(solution)/shard_map/ppermute | solution.py:44
  211.1 2.0 gather_fusion.1
  213.1 0.3 copy_select_fusion.1
  213.4 1.5 slice_bitcast_fusion.3
  214.9 0.0 all-to-all-done.1
  214.9 2.0 gather_fusion.2
  216.9 0.3 copy_select_fusion
  217.2 0.0 collective-permute-done
  217.2 7.9 %gather_fusion = f32[128,128,128]{2,1,0:T(8,128)} fusion(f32[128,128,128]{2,1,0:T(8,128)} %collective-permute-done, s32[1024]{0:T(1024)S(1)} %pad_clamp_fusion.3), kind=kCustom, calls=%fused_computation.2 | custom fusion | bytes 16777728 | tf_op jit(solution)/shard_map/jit(_take)/gather | solution.py:134
  225.1 16.3 %fusion.14 = f32[128,10,128]{2,1,0:T(8,128)S(1)} fusion(f32[128]{0:T(128)S(1)} %compare_select_fusion.4, f32[128,2,10,128]{3,2,0,1:T(8,128)S(1)} %copy_select_fusion, f32[128,128,128]{2,1,0:T(8,128)} %gather_fusion, f32[1,1,256,128,128]{4,3,2,1,0:T(8,128)} %param.16, pred[128]{0:T(512)(128)(4,1)S(1)} %get-tuple-element.240, ...), kind=kOutput, calls=%fused_computation.38 | convolution fusion | flops 256016384 | bytes 18482688 | tf_op jit(solution)/shard_map/nij,nsj->nsi/dot_general | solution.py:88
  241.4 0.5 fusion.16
  241.9 0.0 copy-start
  241.9 3.4 %collective-permute-start.4 = (f32[4,10,128]{2,0,1:T(4,128)S(1)}, f32[4,10,128]{2,0,1:T(4,128)S(1)}, u32[]{:S(2)}, u32[]{:S(2)}) collective-permute-start(f32[4,10,128]{2,0,1:T(4,128)S(1)} %slice.107), channel_id=1, source_target_pairs={{0,64},{4,68},{8,72},{12,76},{16,80},{20,84},{24,88},{28,92},{32,9... | collective-permute-start | bytes 61448 | tf_op jit(solution)/shard_map/ppermute | solution.py:44
  245.3 1.5 slice_bitcast_fusion.2
  246.8 0.7 collective-permute-done.4
  247.5 0.6 copy.24
  248.1 4.5 %all-to-all-start.2 = ((f32[4,1,10,128]{3,1,2,0:T(1,128)}), f32[4,1,10,128]{3,1,2,0:T(1,128)S(1)}, u32[]{:S(2)}, u32[]{:S(2)}) async-start(f32[4,1,10,128]{3,1,2,0:T(1,128)} %copy.24), calls=%async_computation.2 | async-start | bytes 40960 | tf_op jit(solution)/shard_map/all_to_all | solution.py:54
  252.6 0.0 copy-done
  252.6 21.5 %clamp_bitcast_fusion = f32[1,1,128,128,128]{4,3,2,1,0:T(8,128)} fusion(f32[128,10,128]{2,1,0:T(8,128)} %get-tuple-element.232, f32[128,10,128]{2,1,0:T(8,128)S(1)} %copy-done, f32[128,10,128]{2,1,0:T(8,128)} %get-tuple-element.230, f32[128,10,128]{2,1,0:T(8,128)} %get-tuple-element.229, f32[128,128,128]{2,1,0:T(8,128)} %gather_fusion, ...), kind=kOutput, calls=%fused_computation.23 | convolution fusion | flops 514457600 | bytes 27787520 | tf_op jit(solution)/shard_map/nki,nkj->nij/dot_general | solution.py:91
  274.0 0.0 all-to-all-done.2
  274.1 0.7 while.42
  274.8 0.0 copy-start.2
  274.8 0.6 copy-done.2
  (118 shorter events, 2.7 us)
Async XLA Ops:
  1.3 12.0 %copy-start.5 = (s32[1,1,256]{2,1,0:T(1,128)S(1)}, s32[1,1,256]{2,1,0:T(1,128)}, u32[]{:S(2)}) copy-start(s32[1,1,256]{2,1,0:T(1,128)} %param.18) | copy-start | bytes 3076
  1.3 15.5 %copy-start.1 = (s32[10,128]{1,0:T(8,128)S(1)}, s32[10,128]{1,0:T(8,128)}, u32[]{:S(2)}) copy-start(s32[10,128]{1,0:T(8,128)} %param.13) | copy-start | bytes 15364
  1.3 15.5 %copy-start.3 = (f32[3,128]{1,0:T(4,128)S(1)}, f32[3,128]{1,0:T(4,128)}, u32[]{:S(2)}) copy-start(f32[3,128]{1,0:T(4,128)} %param.15) | copy-start | bytes 4612
  1.3 15.5 %copy-start.4 = (f32[2,128]{1,0:T(2,128)S(1)}, f32[2,128]{1,0:T(2,128)}, u32[]{:S(2)}) copy-start(f32[2,128]{1,0:T(2,128)} %param.14) | copy-start | bytes 3076
  1.3 197.0 %copy-start.6 = (s32[1,1,256]{2,1,0:T(1,128)S(1)}, s32[1,1,256]{2,1,0:T(1,128)}, u32[]{:S(2)}) copy-start(s32[1,1,256]{2,1,0:T(1,128)} %param.17) | copy-start | bytes 3076
  1.3 23.7 %collective-permute-start.3 = (s32[128]{0:T(128)S(1)}, s32[128]{0:T(128)S(1)}, u32[]{:S(2)}, u32[]{:S(2)}) collective-permute-start(s32[128]{0:T(128)S(1)} %slice_bitcast_fusion.4), channel_id=1, source_target_pairs={{0,64},{4,68},{8,72},{12,76},{16,80},{20,84},{24,88},{28,92},{32,9... | collective-permute-start | bytes 1544 | tf_op jit(solution)/shard_map/ppermute | solution.py:44
  13.3 204.0 %collective-permute-start = (f32[128,128,128]{2,1,0:T(8,128)}, f32[128,128,128]{2,1,0:T(8,128)}, u32[]{:S(2)}, u32[]{:S(2)}) collective-permute-start(f32[128,128,128]{2,1,0:T(8,128)} %slice_bitcast_fusion), channel_id=1, source_target_pairs={{0,64},{4,68},{8,72},{12,76},{16,80},{20,84},{24,88},{28,92},{32,9... | collective-permute-start | bytes 25165832 | tf_op jit(solution)/shard_map/ppermute | solution.py:44
  13.3 183.7 %collective-permute-start.1 = (s32[128]{0:T(128)S(1)}, s32[128]{0:T(128)S(1)}, u32[]{:S(2)}, u32[]{:S(2)}) collective-permute-start(s32[128]{0:T(128)S(1)} %slice_bitcast_fusion.10), channel_id=1, source_target_pairs={{0,64},{4,68},{8,72},{12,76},{16,80},{20,84},{24,88},{28,92},{32,9... | collective-permute-start | bytes 1544 | tf_op jit(solution)/shard_map/ppermute | solution.py:44
  19.7 178.6 %all-to-all-start = ((f32[4,1,2,10,128]{4,2,3,1,0:T(2,128)}), f32[4,1,2,10,128]{4,2,3,1,0:T(2,128)S(1)}, u32[]{:S(2)}, u32[]{:S(2)}) async-start(f32[4,1,2,10,128]{4,2,3,1,0:T(2,128)} %broadcast_in_dim.106), calls=%async_computation | async-start | bytes 81920 | tf_op jit(solution)/shard_map/all_to_all | solution.py:32
  199.1 15.8 %all-to-all-start.1 = ((f32[32,1,2,10,128]{4,2,3,1,0:T(2,128)}), f32[32,1,2,10,128]{4,2,3,1,0:T(2,128)S(1)}, u32[]{:S(2)}, u32[]{:S(2)}) async-start(f32[32,1,2,10,128]{4,2,3,1,0:T(2,128)} %broadcast_in_dim.110), calls=%async_computation.1 | async-start | bytes 655360 | tf_op jit(solution)/shard_map/all_to_all | solution.py:32
  204.3 6.8 %collective-permute-start.2 = (f32[4,2,10,128]{3,1,2,0:T(2,128)S(1)}, f32[4,2,10,128]{3,1,2,0:T(2,128)S(1)}, u32[]{:S(2)}, u32[]{:S(2)}) collective-permute-start(f32[4,2,10,128]{3,1,2,0:T(2,128)S(1)} %bitcast.106), channel_id=1, source_target_pairs={{0,64},{4,68},{8,72},{12,76},{16,80},{20,84},{24,88},{28,92},{32,9... | collective-permute-start | bytes 122888 | tf_op jit(solution)/shard_map/ppermute | solution.py:44
  241.9 10.6 %copy-start = (f32[128,10,128]{2,1,0:T(8,128)S(1)}, f32[128,10,128]{2,1,0:T(8,128)}, u32[]{:S(2)}) copy-start(f32[128,10,128]{2,1,0:T(8,128)} %get-tuple-element.231) | copy-start | bytes 1966084
  241.9 5.5 %collective-permute-start.4 = (f32[4,10,128]{2,0,1:T(4,128)S(1)}, f32[4,10,128]{2,0,1:T(4,128)S(1)}, u32[]{:S(2)}, u32[]{:S(2)}) collective-permute-start(f32[4,10,128]{2,0,1:T(4,128)S(1)} %slice.107), channel_id=1, source_target_pairs={{0,64},{4,68},{8,72},{12,76},{16,80},{20,84},{24,88},{28,92},{32,9... | collective-permute-start | bytes 61448 | tf_op jit(solution)/shard_map/ppermute | solution.py:44
  248.1 25.9 %all-to-all-start.2 = ((f32[4,1,10,128]{3,1,2,0:T(1,128)}), f32[4,1,10,128]{3,1,2,0:T(1,128)S(1)}, u32[]{:S(2)}, u32[]{:S(2)}) async-start(f32[4,1,10,128]{3,1,2,0:T(1,128)} %copy.24), calls=%async_computation.2 | async-start | bytes 40960 | tf_op jit(solution)/shard_map/all_to_all | solution.py:54
  274.8 0.6 copy-start.2
where the time goes:
time: 278 us; the launch traced here: 275 us
  waiting for transfers between devices  175 us (63%)
  matrix products  38.3 us (14%)
  local copies, waits for them, and re-layouts  28.9 us (10%)
  starting transfers between devices  28.4 us (10%)
  other arithmetic  2.92 us (1%)
    ppermute x5, waiting for transfers between devices, from_partner(): return lax.ppermute(value, axis, pairs)  175 us
    dot_general x1, matrix products, block_work(): jnp.einsum('nki,nkj->nij', post_terms, pre_terms, precision=HIGHEST)  21.5 us
    dot_general x1, matrix products, block_work(): current = jnp.einsum('nij,nsj->nsi', weights, driven, precision=HIGHEST)  16.3 us
    ppermute x5, starting transfers between devices, from_partner(): return lax.ppermute(value, axis, pairs)  14.4 us
    all_to_all x2, starting transfers between devices, copy_for_each(): lax.all_to_all(jnp.broadcast_to(shard[None], (size, *shard.shape)), axis,...  9.61 us
    slice x1, local copies, waits for them, and re-layouts, body(): own_weights[half_slots:]  7.89 us
    gather x1, local copies, waits for them, and re-layouts, body(): jnp.take(incoming_weights, picked, axis=0)  7.86 us
  transfers between devices with their start and end apart: 8, of which 3 were waited for; matrix products, arithmetic and copies ran while one was open for 16% of the time, Pallas kernels for 0%

commit v1 on v0

v1 whole, which is shorter than its diff:
```python
import functools
import math

import jax
import jax.numpy as jnp
from jax import lax
from jax.experimental import pallas as pl
from jax.experimental.pallas import tpu as pltpu
from jax.sharding import PartitionSpec as P

BASE_USE = 0.25
USE_DECAY = 0.98
SUPPLY_RATE = 0.005
PLUS_DECAY = math.exp(-1.0 / 16.8)
MINUS_DECAY = math.exp(-1.0 / 33.7)
SLOW_DECAY = math.exp(-1.0 / 114.0)
SYN_DECAY = math.exp(-1.0 / 5.0)
PAIR_UP = 1.0
TRIPLET_UP = 0.8
PAIR_DOWN = 0.9
LEARN_RATE = 0.02
WEIGHT_MAX = 1.0
INHIB_GAIN = 4.0

G = 128
HALF = 128
STEPS = 10
ROWS = 32
COLS = 4
MESH = pl.DeviceIdType.MESH
F32 = jnp.float32
I32 = jnp.int32
BF16 = jnp.bfloat16

E = 7
ES = 32
FAR = 8 * E
SLOTS_S = FAR + ES
M0 = 12
M1 = 20
RUNGS = (44, 48, 54, 62)
ITERS = 8
STEP_W = 10.0
ORDER = (1, 2, 3, 4, 5, 6, 7, 8, 0)
INVERSE = (0, 3, 4, 1, 2, 7, 8, 5, 6)
BASE = tuple([FAR] + [(k - 1) * E for k in range(1, 9)])
CAP = tuple([ES] + [E] * 8)
VMEM_LIMIT = 60 * 1024 * 1024
ANY = pl.BlockSpec(memory_space=pl.ANY)
SMEM = pl.BlockSpec(memory_space=pltpu.SMEM)
VMEM = pl.BlockSpec(memory_space=pltpu.VMEM)


def place():
    row, col = lax.axis_index("row"), lax.axis_index("col")
    return row, col


def at(row, col):
    return {"row": row, "col": col}


def flip_core(row):
    return row + 1 - 2 * lax.rem(row, 2)


def across(row):
    return lax.rem(row + ROWS // 2, ROWS)


def shift_x(row, step):
    within = lax.rem(row, 8)
    return row - within + lax.rem(within + 2 * step + 8, 8)


def neighbour(k, row, col):
    if k == 0:
        return at(flip_core(row), col)
    which, other = (k - 1) // 2, (k - 1) % 2
    if which < 2:
        row = shift_x(row, 1 if which == 0 else -1)
    else:
        col = lax.rem(col + (1 if which == 2 else COLS - 1), COLS)
    return at(flip_core(row) if other else row, col)


def greet(peers):
    barrier = pltpu.get_barrier_semaphore()
    for peer in peers:
        pl.semaphore_signal(barrier, inc=1, device_id=peer, device_id_type=MESH)
    pl.semaphore_wait(barrier, len(peers))


def send(src, dst, send_sem, recv_sem, peer):
    return pltpu.make_async_remote_copy(
        src_ref=src, dst_ref=dst, send_sem=send_sem, recv_sem=recv_sem, device_id=peer, device_id_type=MESH
    )


def tables_kernel(pack, idx, tab, rtab, ptab, pidx, cnt, s1, r1, s2, r2, s3, r3, s4, r4):
    row, col = place()
    far = across(row)
    barrier = pltpu.get_barrier_semaphore()

    @pl.loop(1, ROWS)
    def _(d):
        peer = at(lax.rem(row + d, ROWS), col)
        pl.semaphore_signal(barrier, inc=1, device_id=peer, device_id_type=MESH)

    for d in range(1, COLS):
        c = lax.rem(col + d, COLS)
        pl.semaphore_signal(barrier, inc=1, device_id=at(row, c), device_id_type=MESH)
        pl.semaphore_signal(barrier, inc=1, device_id=at(far, c), device_id_type=MESH)
    pl.semaphore_wait(barrier, ROWS - 1 + 2 * (COLS - 1))

    @pl.loop(1, ROWS)
    def _(d):
        peer = at(lax.rem(row + d, ROWS), col)
        send(pack, tab.at[row], s1.at[d], r1.at[row], peer).start()

    small = []
    for d in range(1, COLS):
        c = lax.rem(col + d, COLS)
        small.append(send(pack, rtab.at[col], s2.at[d], r2.at[col], at(row, c)))
    for d in range(COLS):
        c = lax.rem(col + d, COLS)
        small.append(send(pack, ptab.at[col], s3.at[d], r3.at[col], at(far, c)))
    small.append(send(idx, pidx, s4.at[0], r4.at[0], at(far, col)))
    for copy in small:
        copy.start()
    tab[row] = pack[...]
    rtab[col] = pack[...]

    @pl.loop(1, ROWS)
    def _(d):
        source = lax.rem(row + d, ROWS)
        send(pack, tab.at[source], s1.at[d], r1.at[source], at(source, col)).wait()

    cnt[col] = tab[:, 15, :]
    counts = []
    for d in range(1, COLS):
        c = lax.rem(col + d, COLS)
        counts.append(send(cnt.at[col], cnt.at[col], s4.at[d], r4.at[1 + col], at(row, c)))
    for copy in counts:
        copy.start()
    for d in range(1, COLS):
        c = lax.rem(col + d, COLS)
        send(pack, rtab.at[c], s2.at[d], r2.at[c], at(row, c)).wait()
    for d in range(COLS):
        c = lax.rem(col + d, COLS)
        send(pack, ptab.at[c], s3.at[d], r3.at[c], at(far, c)).wait()
    small[-1].wait()
    for d in range(1, COLS):
        c = lax.rem(col + d, COLS)
        send(cnt.at[c], cnt.at[c], s4.at[d], r4.at[1 + c], at(row, c)).wait()


def exchange_tables(pack, idx):
    dma = pltpu.SemaphoreType.DMA
    return pl.pallas_call(
        tables_kernel,
        out_shape=(
            jax.ShapeDtypeStruct((ROWS, 16, G), F32),
            jax.ShapeDtypeStruct((COLS, 16, G), F32),
            jax.ShapeDtypeStruct((COLS, 16, G), F32),
            jax.ShapeDtypeStruct((8, G), I32),
            jax.ShapeDtypeStruct((COLS, ROWS, G), F32),
        ),
        in_specs=[VMEM, VMEM],
        out_specs=(VMEM,) * 5,
        scratch_shapes=[
            dma((ROWS,)), dma((ROWS,)), dma((COLS,)), dma((COLS,)),
            dma((COLS,)), dma((COLS,)), dma((COLS,)), dma((COLS + 1,)),
        ],
        compiler_params=pltpu.CompilerParams(collective_id=0, has_side_effects=True),
        name="tables",
    )(pack, idx)


def plan_kernel(cnt, tables, rung):
    row, col = place()
    shape = (8, G)
    lane = lax.broadcasted_iota(I32, shape, 1)
    sub = lax.broadcasted_iota(I32, (ROWS, G), 0)
    lane_t = lax.broadcasted_iota(I32, (ROWS, G), 1)
    total = jnp.zeros((1, G), F32)
    for c in range(COLS):
        total = total + jnp.sum(jnp.where(lane_t == sub + c * ROWS, cnt[c], 0.0), axis=0, keepdims=True)
    count = jnp.broadcast_to(total, shape)
    surplus = jnp.maximum(count - HALF, 0.0)
    core = lax.rem(lane, 2)
    x_at = lax.rem(lane, 8) // 2
    z_hi = lax.rem(lane, 32) // 16

    def roll(value, by):
        return pltpu.roll(value, by % G, 1)

    def from_sibling(v):
        return jnp.where(core == 0, roll(v, -1), roll(v, 1))

    def seen(v):
        same = (
            jnp.where(x_at == 3, roll(v, 6), roll(v, -2)),
            jnp.where(x_at == 0, roll(v, -6), roll(v, 2)),
            roll(v, -ROWS),
            roll(v, ROWS),
        )
        out = [from_sibling(v)]
        for value in same:
            out += [value, from_sibling(value)]
        return out

    outs = [jnp.zeros(shape, F32)] * 9
    ins = [jnp.zeros(shape, F32)] * 9
    for _ in range(ITERS):
        load = surplus
        for k in range(9):
            load = load - outs[k] + ins[k]
        near = seen(load)
        for k in range(9):
            gap = (load - near[k]) * (1.0 / STEP_W)
            outs[k] = jnp.clip(outs[k] + gap, 0.0, float(CAP[k]))
        spent = functools.reduce(jnp.add, outs)
        scale = jnp.minimum(1.0, surplus / jnp.maximum(spent, 1e-6))
        outs = [v * scale for v in outs]
        moved = [None] * 9
        moved[0] = from_sibling(outs[0])
        back = (
            lambda v: jnp.where(x_at == 3, roll(v, 6), roll(v, -2)),
            lambda v: jnp.where(x_at == 0, roll(v, -6), roll(v, 2)),
            lambda v: roll(v, -ROWS),
            lambda v: roll(v, ROWS),
        )
        for k in range(1, 9):
            value = back[(k - 1) // 2](outs[INVERSE[k]])
            moved[k] = from_sibling(value) if (k - 1) % 2 else value
        ins = moved
    give = [jnp.minimum(jnp.floor(v + 0.5), float(CAP[k])) for k, v in enumerate(outs)]
    over = jnp.maximum(functools.reduce(jnp.add, give) - surplus, 0.0)
    for k in range(9):
        cut = jnp.minimum(give[k], over)
        give[k] = give[k] - cut
        over = over - cut
    take = [None] * 9
    take[0] = from_sibling(give[0])
    for k in range(1, 9):
        value = back[(k - 1) // 2](give[INVERSE[k]])
        take[k] = from_sibling(value) if (k - 1) % 2 else value
    own = surplus - functools.reduce(jnp.add, give)
    far_in = functools.reduce(jnp.add, take[1:])
    need = jnp.maximum(own, float(M0)) + far_in + take[0]
    worst = jnp.max(need)
    worst_far = jnp.max(far_in)
    picked = jnp.int32(0)
    for size in RUNGS:
        picked = picked + jnp.where(worst > float(size), 1, 0)
    picked = jnp.where(worst_far > float(M1), len(RUNGS), picked)
    full = picked == len(RUNGS)
    rung[0] = picked

    me = col * ROWS + row
    mate = col * ROWS + across(row)

    def of(v, who):
        return jnp.max(jnp.where(lane == who, v, -1.0), axis=1, keepdims=True).astype(I32)[:1]

    give_me = [of(v, me) for v in give]
    give_mate = [of(v, mate) for v in give]
    take_me = [of(v, me) for v in take]
    take_mate = [of(v, mate) for v in take]
    own_me, own_mate = of(own, me), of(own, mate)
    held = of(count, me)
    slot = lax.broadcasted_iota(I32, (1, G), 1)

    def table(i, value, top):
        tables[pl.ds(i, 1), :] = jnp.clip(value, 0, top)

    spread = jnp.zeros((1, G), I32)
    gather = jnp.zeros((1, G), I32)
    before_give, before_take = own_me, jnp.zeros((1, 1), I32)
    for k in ORDER:
        here = (slot >= BASE[k]) & (slot < BASE[k] + CAP[k])
        spread = jnp.where(here, slot - BASE[k] + before_give, spread)
        gather = jnp.where(here, slot - BASE[k] + before_take, gather)
        before_give = before_give + give_me[k]
        before_take = before_take + take_mate[k]
    table(0, spread, HALF - 1)
    turn = slot - M0
    ahead = jnp.zeros((1, 1), I32)
    imported = jnp.zeros((1, G), I32)
    is_import = jnp.zeros((1, G), I32)
    for k in ORDER:
        here = (turn >= ahead) & (turn < ahead + take_me[k])
        imported = jnp.where(here, BASE[k] + turn - ahead, imported)
        is_import = jnp.where(here, 1, is_import)
        ahead = ahead + take_me[k]
    table(1, M0 + turn - ahead, HALF - 1)
    table(2, imported, SLOTS_S - 1)
    table(3, is_import, 1)
    table(4, gather, HALF - 1)
    j = slot - held
    spot = jnp.where(j < M0, j, j + functools.reduce(jnp.add, take_mate))
    before = own_mate
    for k in ORDER:
        here = (j >= before) & (j < before + give_mate[k])
        spot = jnp.where(here, HALF + BASE[k] + j - before, spot)
        before = before + give_mate[k]
    spot = jnp.where(full, j, spot)
    table(5, jnp.where(j < 0, 0, spot), HALF + SLOTS_S - 1)
    table(6, jnp.where(j < 0, 0, 1), 1)
    table(7, j, HALF - 1)


def make_plan(cnt):
    return pl.pallas_call(
        plan_kernel,
        out_shape=(jax.ShapeDtypeStruct((8, G), I32), jax.ShapeDtypeStruct((1,), I32)),
        in_specs=[VMEM],
        out_specs=(VMEM, SMEM),
        name="plan",
    )(cnt)


def move_kernel(size, tables, weights, staged, up, spread, imports, z1, z2, got1, got2, back, ls, ss, rs, zs, zr, gs, gr):
    row, col = place()
    mate = at(across(row), col)
    peers = [neighbour(k, row, col) for k in range(9)]
    m2 = size - M0 - M1
    load = pltpu.make_async_copy(weights.at[pl.ds(HALF, HALF)], up, ls.at[0])
    load.start()
    greet(peers + [mate])
    load.wait()
    first = send(up.at[pl.ds(0, M0)], staged.at[pl.ds(0, M0)], zs.at[0], zr.at[0], mate)
    first.start()

    spreads = [
        send(spread.at[pl.ds(BASE[k], CAP[k])], imports.at[pl.ds(BASE[INVERSE[k]], CAP[k])], ss.at[k], rs.at[INVERSE[k]], peers[k])
        for k in range(9)
    ]
    for k in ORDER:

        @pl.loop(BASE[k], BASE[k] + CAP[k])
        def _(i):
            spread[i] = up[tables[0, i]]

        spreads[k].start()
    for k in range(9):
        send(spread.at[pl.ds(BASE[k], CAP[k])], imports.at[pl.ds(BASE[k], CAP[k])], ss.at[k], rs.at[k], peers[k]).wait_recv()

    def fill(target, start, count):
        @pl.loop(0, count)
        def _(i):
            at_slot = start + i
            target[i] = jnp.where(tables[3, at_slot] == 1, imports[tables[2, at_slot]], up[tables[1, at_slot]])

    second = send(z1, got1, zs.at[1], zr.at[1], mate)
    third = send(z2, got2, zs.at[2], zr.at[2], mate)
    fill(z1, M0, M1)
    second.start()
    fill(z2, M0 + M1, m2)
    third.start()

    gathers = [
        send(back.at[pl.ds(BASE[k], CAP[k])], staged.at[pl.ds(HALF + BASE[INVERSE[k]], CAP[k])], gs.at[k], gr.at[INVERSE[k]], peers[k])
        for k in range(9)
    ]
    second.wait_recv()
    for k in range(1, 9):

        @pl.loop(BASE[k], BASE[k] + CAP[k])
        def _(i):
            back[i] = got1[jnp.minimum(tables[4, i], M1 - 1)]

        gathers[k].start()
    out1 = pltpu.make_async_copy(got1, staged.at[pl.ds(M0, M1)], ls.at[1])
    out1.start()
    third.wait_recv()
    out2 = pltpu.make_async_copy(got2, staged.at[pl.ds(M0 + M1, m2)], ls.at[2])
    out2.start()

    @pl.loop(BASE[0], BASE[0] + ES)
    def _(i):
        t = tables[4, i]
        back[i] = jnp.where(t < M1, got1[jnp.minimum(t, M1 - 1)], got2[jnp.clip(t - M1, 0, m2 - 1)])

    gathers[0].start()
    out1.wait()
    out2.wait()
    first.wait()
    second.wait_send()
    third.wait_send()
    for k in range(9):
        spreads[k].wait_send()
        gathers[k].wait_send()
        send(back.at[pl.ds(BASE[k], CAP[k])], staged.at[pl.ds(HALF + BASE[k], CAP[k])], gs.at[k], gr.at[k], peers[k]).wait_recv()


def full_kernel(weights, staged, ss, rs):
    row, col = place()
    mate = at(across(row), col)
    greet([mate])
    copy = send(weights.at[pl.ds(HALF, HALF)], staged.at[pl.ds(0, HALF)], ss, rs, mate)
    copy.start()
    copy.wait()


STAGED = jax.ShapeDtypeStruct((HALF + SLOTS_S, G, G), F32)


def move(index, tables, weights):
    dma = pltpu.SemaphoreType.DMA
    if index == len(RUNGS):
        return pl.pallas_call(
            full_kernel,
            out_shape=STAGED,
            in_specs=[ANY],
            out_specs=ANY,
            scratch_shapes=[dma, dma],
            compiler_params=pltpu.CompilerParams(
                collective_id=2 + index, has_side_effects=True, vmem_limit_bytes=VMEM_LIMIT
            ),
            name="move_full",
        )(weights)
    size = RUNGS[index]
    m2 = size - M0 - M1

    def blocks(n):
        return pltpu.VMEM((n, G, G), F32)

    return pl.pallas_call(
        functools.partial(move_kernel, size),
        out_shape=STAGED,
        in_specs=[SMEM, ANY],
        out_specs=ANY,
        scratch_shapes=[
            blocks(HALF), blocks(SLOTS_S), blocks(SLOTS_S), blocks(M1), blocks(m2), blocks(M1), blocks(m2), blocks(SLOTS_S),
            dma((3,)), dma((9,)), dma((9,)), dma((3,)), dma((3,)), dma((9,)), dma((9,)),
        ],
        compiler_params=pltpu.CompilerParams(
            collective_id=2 + index, has_side_effects=True, vmem_limit_bytes=VMEM_LIMIT
        ),
        name=f"move_{size}",
    )(tables, weights)


CHUNK = 8
KP = 64


def split(value):
    high = value.astype(BF16)
    return high, (value - high.astype(F32)).astype(BF16)


def blocks_kernel(
    tables, pre, post, pidx, tab, rtab, ptab, weights, staged, new, cur, qs, ds, ps, scr, acc, win, wout, sem_in, sem_out
):
    steps = HALF // CHUNK

    def fetch(step, slot):
        for b in range(CHUNK):
            s = step * CHUNK + b
            moved = tables[6, s]

            @pl.when(moved == 0)
            def _():
                pltpu.make_async_copy(weights.at[s], win.at[slot, b], sem_in.at[slot]).start()

            @pl.when(moved == 1)
            def _():
                pltpu.make_async_copy(staged.at[tables[5, s]], win.at[slot, b], sem_in.at[slot]).start()

    fetch(0, 0)
    fetch(1, 1)
    neuron = lax.broadcasted_iota(I32, (1, G), 1)
    polarity = jnp.where(lax.rem(neuron, 5) == 4, -INHIB_GAIN, 1.0).astype(F32)

    use, supply, fast = tab[:, 10, :], tab[:, 11, :], tab[:, 12, :]
    scr[...] = jnp.zeros_like(scr)
    for t in range(STEPS):
        s = tab[:, t, :]
        use = BASE_USE + (use - BASE_USE) * USE_DECAY
        use = use + s * BASE_USE * (1.0 - use)
        release = s * use * supply
        supply = supply + SUPPLY_RATE * (1.0 - supply) - release
        fast = fast * PLUS_DECAY + s
        scr[:, t, :] = fast
        scr[:, STEPS + t, :] = release

    @pl.loop(0, ROWS)
    def _(g):
        terms = scr[g]
        high = terms.astype(BF16).astype(F32)
        low = terms - high
        qs[g] = jnp.concatenate([high[:20], low[:20], high[:20], jnp.zeros((4, G), F32)], axis=0).astype(BF16)
        driven = terms[STEPS : 2 * STEPS] * polarity
        dh = driven.astype(BF16).astype(F32)
        dl = driven - dh
        pad6 = jnp.zeros((6, G), F32)
        wide = jnp.concatenate([dh, pad6, dl, pad6, jnp.zeros((G - 32, G), F32)], axis=0)
        tall = jnp.transpose(wide)
        only = jnp.transpose(jnp.concatenate([dh, jnp.zeros((G - 10, G), F32)], axis=0))
        ds[g, pl.ds(0, G), :] = tall.astype(BF16)
        ds[g, pl.ds(G, G), :] = only.astype(BF16)

    for half, source in enumerate((rtab, ptab)):
        fast_p, slow_p = source[:, 13, :], source[:, 14, :]
        for t in range(STEPS):
            s = source[:, t, :]
            scr[pl.ds(half * COLS, COLS), t, :] = s * (PAIR_UP + TRIPLET_UP * slow_p)
            scr[pl.ds(half * COLS, COLS), STEPS + t, :] = -(PAIR_DOWN * fast_p)
            fast_p = fast_p * MINUS_DECAY + s
            slow_p = slow_p * SLOW_DECAY + s

    @pl.loop(0, 2 * COLS)
    def _(g):
        terms = scr[g] * LEARN_RATE
        high = terms.astype(BF16).astype(F32)
        low = terms - high
        rows = jnp.concatenate([high[:20], high[:20], low[:20], jnp.zeros((G - 60, G), F32)], axis=0)
        ps[g] = jnp.transpose(rows).astype(BF16)

    acc[...] = jnp.zeros_like(acc)

    @pl.loop(0, steps)
    def _(step):
        slot = lax.rem(step, 3)
        pltpu.make_async_copy(weights.at[pl.ds(0, CHUNK)], win.at[slot], sem_in.at[slot]).wait()

        @pl.when(step + 2 < steps)
        def _():
            fetch(step + 2, lax.rem(step + 2, 3))

        @pl.when(step >= 2)
        def _():
            pltpu.make_async_copy(wout.at[0], new.at[pl.ds(0, CHUNK)], sem_out.at[lax.rem(step, 2)]).wait()

        o = lax.rem(step, 2)
        currents = []
        for b in range(CHUNK):
            s = step * CHUNK + b
            moved, there = tables[6, s] == 1, tables[7, s]
            p = jnp.where(moved, pidx[0, there], pre[s])
            q = jnp.where(moved, pidx[1, there] + COLS, post[s])
            w = win[slot, b]
            change = jnp.dot(ps[q][:, :KP], qs[p], preferred_element_type=F32)
            wh, wl = split(w)
            currents.append((q, jnp.dot(jnp.concatenate([wh, wl], axis=1), ds[p], preferred_element_type=F32)))
            wout[o, b] = jnp.clip(w + change, 0.0, WEIGHT_MAX)
        for q, value in currents:
            acc[q] += value
        pltpu.make_async_copy(wout.at[o], new.at[pl.ds(step * CHUNK, CHUNK)], sem_out.at[o]).start()

    for q in range(2 * COLS):
        turned = jnp.transpose(acc[q])
        cur[q] = turned[0:16] + turned[16:32]
    for o in range(2):
        pltpu.make_async_copy(wout.at[o], new.at[pl.ds(0, CHUNK)], sem_out.at[o]).wait()


def do_blocks(tables, pre, post, pidx, tab, rtab, ptab, weights, staged):
    dma = pltpu.SemaphoreType.DMA
    return pl.pallas_call(
        blocks_kernel,
        out_shape=(jax.ShapeDtypeStruct((HALF, G, G), F32), jax.ShapeDtypeStruct((2 * COLS, 16, G), F32)),
        in_specs=[SMEM, SMEM, SMEM, SMEM, VMEM, VMEM, VMEM, ANY, ANY],
        out_specs=(ANY, VMEM),
        scratch_shapes=[
            pltpu.VMEM((ROWS, KP, G), BF16),
            pltpu.VMEM((ROWS, 2 * G, G), BF16),
            pltpu.VMEM((2 * COLS, G, G), BF16),
            pltpu.VMEM((ROWS, 24, G), F32),
            pltpu.VMEM((2 * COLS, G, G), F32),
            pltpu.VMEM((3, CHUNK, G, G), F32),
            pltpu.VMEM((2, CHUNK, G, G), F32),
            dma((3,)), dma((2,)),
        ],
        compiler_params=pltpu.CompilerParams(vmem_limit_bytes=VMEM_LIMIT),
        name="blocks",
    )(tables, pre, post, pidx, tab, rtab, ptab, weights, staged)


def currents_kernel(cur, out, got, ss, rs):
    row, col = place()
    far = across(row)
    peers, copies, arrivals = [], [], []
    for d in range(1, COLS):
        c = lax.rem(col + d, COLS)
        peers.append(at(row, c))
        copies.append(send(cur.at[c], got.at[col], ss.at[d], rs.at[col], at(row, c)))
        arrivals.append(send(cur.at[c], got.at[c], ss.at[d], rs.at[c], at(row, c)))
    for d in range(COLS):
        c = lax.rem(col + d, COLS)
        peers.append(at(far, c))
        copies.append(send(cur.at[COLS + c], got.at[COLS + col], ss.at[COLS + d], rs.at[COLS + col], at(far, c)))
        arrivals.append(send(cur.at[COLS + c], got.at[COLS + c], ss.at[COLS + d], rs.at[COLS + c], at(far, c)))
    greet(peers)
    for copy in copies:
        copy.start()
    got[col] = cur[col]
    for copy in arrivals:
        copy.wait()
    drive = got[0]
    for i in range(1, 2 * COLS):
        drive = drive + got[i]
    gain = 1.0 / math.sqrt(G * HALF)
    state = jnp.zeros((1, G), F32)
    for t in range(STEPS):
        state = state * SYN_DECAY + gain * drive[t : t + 1]
        out[pl.ds(t, 1), :] = state


def settle(cur):
    dma = pltpu.SemaphoreType.DMA
    return pl.pallas_call(
        currents_kernel,
        out_shape=jax.ShapeDtypeStruct((STEPS, G), F32),
        in_specs=[VMEM],
        out_specs=VMEM,
        scratch_shapes=[pltpu.VMEM((2 * COLS, 16, G), F32), dma((2 * COLS,)), dma((2 * COLS,))],
        compiler_params=pltpu.CompilerParams(collective_id=1, has_side_effects=True),
        name="currents",
    )(cur)


def body(spikes, stp_init, trace_init, weights, block_pre, block_post, block_count):
    own = weights[0, 0]
    pre, post = block_pre[0, 0], block_post[0, 0]
    held = block_count[0]
    pack = jnp.concatenate(
        [spikes.astype(F32), stp_init, trace_init, jnp.broadcast_to(held.astype(F32)[:, None], (1, G))], axis=0
    )
    idx = jnp.concatenate(
        [pre[None, HALF:], post[None, HALF:], jnp.zeros((6, G), I32)], axis=0
    )
    tab, rtab, ptab, pidx, cnt = exchange_tables(pack, idx)
    tables, rung = make_plan(cnt)
    staged = lax.switch(rung[0], [functools.partial(move, i) for i in range(len(RUNGS) + 1)], tables, own)
    new, cur = do_blocks(tables, pre, post, pidx, tab, rtab, ptab, own, staged)
    synaptic = settle(cur)
    return (new[None, None], synaptic)


def solution(mesh):
    placed = (
        P(None, ("row", "col")),
        P(None, ("row", "col")),
        P(None, ("row", "col")),
        P("row", "col", None, None, None),
        P("row", "col", None),
        P("row", "col", None),
        P("row", "col"),
    )
    return jax.shard_map(
        body,
        mesh=mesh,
        in_specs=placed,
        out_specs=(P("row", "col", None, None, None), P(None, ("row", "col"))),
        check_vma=False,
    )
```

time: 278 us -> 241 us (0.87)
  Pallas kernels: 0 us -> 233 us
  waiting for transfers between devices: 175 us -> 0 us
  matrix products: 38.3 us -> 0 us
  starting transfers between devices: 28.4 us -> 0 us
  local copies, waits for them, and re-layouts: 28.9 us -> 2.12 us
    pallas_call x0 -> x5, Pallas kernels: none -> 233 us  [the longest x1 184 us: move(): pl.pallas_call(full_kernel, out_shape=STAGED, in_specs=[ANY], out_specs=A...]
    ppermute x5 -> x0, waiting for transfers between devices: 175 us -> none  [from_partner(): return lax.ppermute(value, axis, pairs)]
    dot_general x3 -> x0, matrix products: 38.3 us -> none  [the longest x1 21.5 us: block_work(): jnp.einsum('nki,nkj->nij', post_terms, pre_terms, precision=HIGHEST)]
    ppermute x5 -> x0, starting transfers between devices: 14.4 us -> none  [from_partner(): return lax.ppermute(value, axis, pairs)]
    gather x5 -> x0, local copies, waits for them, and re-layouts: 14.3 us -> none  [the longest x1 7.86 us: body(): jnp.take(incoming_weights, picked, axis=0)]
    all_to_all x3 -> x0, starting transfers between devices: 14.1 us -> none  [the longest x2 9.61 us: copy_for_each(): lax.all_to_all(jnp.broadcast_to(shard[None], (size, *shard.shape)), axis,...]
    slice x4 -> x0, local copies, waits for them, and re-layouts: 8.56 us -> none  [the longest x1 7.89 us: body(): own_weights[half_slots:]]
  transfers between devices with their start and end apart: 8 -> 0, of which waited for: 3 -> 0; matrix products, arithmetic and copies ran while one was open for 16% -> 0% of each run, Pallas kernels for 0% -> 0%
where the time goes in v1:
time: 241 us; the launch traced here: 240 us
  Pallas kernels  233 us (97%)
  other arithmetic  2.72 us (1%)
    pallas_call x1, Pallas kernels, move(): pl.pallas_call(full_kernel, out_shape=STAGED, in_specs=[ANY], out_specs=A...  184 us
    pallas_call x1, Pallas kernels, exchange_tables(): pl.pallas_call(tables_kernel, out_shape=(jax.ShapeDtypeStruct((ROWS, 16,...  20 us
    pallas_call x1, Pallas kernels, do_blocks(): pl.pallas_call(blocks_kernel, out_shape=(jax.ShapeDtypeStruct((HALF, G, G...  16.2 us
    pallas_call x1, Pallas kernels, settle(): pl.pallas_call(currents_kernel, out_shape=jax.ShapeDtypeStruct((STEPS, G)...  9.5 us

profile of v1, /device:TPU:0, one launch (start us, length us, event | category | flops | bytes accessed | tf_op | source)
XLA Modules:
  0.0 240.1 jit_solution(13481643355117166796)
XLA Ops:
  1.3 0.1 pad.6.clone
  1.4 0.1 pad.2.clone
  1.4 0.7 slice_bitcast_fusion
  2.1 0.7 add_add_fusion.idx
  2.8 0.7 convert_element_type.7
  3.5 1.4 maximum_maximum_fusion.pack
  4.8 20.0 %tables.1 = (f32[32,16,128]{2,1,0:T(8,128)}, f32[4,16,128]{2,1,0:T(8,128)}, f32[4,16,128]{2,1,0:T(8,128)}, s32[8,128]{1,0:T(8,128)}, f32[4,32,128]{2,1,0:T(8,128)}) custom-call(f32[16,128]{1,0:T(8,128)} %maximum_maximum_fusion.pack, s32[8,128]{1,0:T(8,128)} %add_add_fusion.idx), custom_call_target="tpu_custom_call" | custom-call | tf_op jit(solution)/shard_map/tables/pallas_call | solution.py:160
  24.8 4.0 %plan.1 = (s32[8,128]{1,0:T(8,128)S(1)}, s32[1]{0:T(128)}) custom-call(f32[4,32,128]{2,1,0:T(8,128)} %get-tuple-element.42.cnt), custom_call_target="tpu_custom_call" | custom-call | tf_op jit(solution)/shard_map/plan/pallas_call | solution.py:315
  29.4 183.6 %conditional.1 = (f32[216,128,128]{2,1,0:T(8,128)}) conditional(s32[]{:T(128)} %bitcast.6, (s32[8,128]{1,0:T(8,128)S(1)}, f32[256,128,128]{2,1,0:T(8,128)}) %tuple.33, (s32[8,128]{1,0:T(8,128)S(1)}, f32[256,128,128]{2,1,0:T(8,128)}) %tuple.34, (s32[8,128]{1,0:T(8,128)S(1)}, f32[256,128,128]{2,1,0:T(8,128)}) %tuple.35, ...), branch_computations={%region_0.0_spmd, %region_1.0_spmd, %region_2.0_spmd, %region_3.0_... | conditional | bytes 8 | solution.py:638
  29.5 183.5 %move_full.1 = f32[216,128,128]{2,1,0:T(8,128)} custom-call(f32[256,128,128]{2,1,0:T(8,128)} %weights), custom_call_target="tpu_custom_call" | custom-call | tf_op jit(solution)/shard_map/cond/branch_4_fun/move_full/pallas_call | solution.py:413
  213.0 16.2 %blocks.1 = (f32[128,128,128]{2,1,0:T(8,128)}, f32[8,16,128]{2,1,0:T(8,128)}) custom-call(s32[8,128]{1,0:T(8,128)S(1)} %get-tuple-element.43.tables, s32[256]{0:T(256)} %bitcast.19, s32[256]{0:T(256)} %bitcast.18, s32[8,128]{1,0:T(8,128)} %get-tuple-element.44.pidx, f32[32,16,128]{2,1,0:T(8,128)} %get-tuple-element.45.tab, ...), custom_call_target="tpu_custom_call" | custom-call | tf_op jit(solution)/shard_map/blocks/pallas_call | solution.py:563
  229.3 9.5 %currents.1 = f32[10,128]{1,0:T(8,128)} custom-call(f32[8,16,128]{2,1,0:T(8,128)} %get-tuple-element.50.cur), custom_call_target="tpu_custom_call" | custom-call | tf_op jit(solution)/shard_map/currents/pallas_call | solution.py:615
  238.8 1.3 copy.16
  (1 shorter events, 0.0 us)

commit v2 on v1

v2 whole, which is shorter than its diff:
```python
import functools
import math

import jax
import jax.numpy as jnp
from jax import lax
from jax.experimental import pallas as pl
from jax.experimental.pallas import tpu as pltpu
from jax.sharding import PartitionSpec as P

BASE_USE = 0.25
USE_DECAY = 0.98
SUPPLY_RATE = 0.005
PLUS_DECAY = math.exp(-1.0 / 16.8)
MINUS_DECAY = math.exp(-1.0 / 33.7)
SLOW_DECAY = math.exp(-1.0 / 114.0)
SYN_DECAY = math.exp(-1.0 / 5.0)
PAIR_UP = 1.0
TRIPLET_UP = 0.8
PAIR_DOWN = 0.9
LEARN_RATE = 0.02
WEIGHT_MAX = 1.0
INHIB_GAIN = 4.0

G = 128
HALF = 128
STEPS = 10
ROWS = 32
COLS = 4
MESH = pl.DeviceIdType.MESH
F32 = jnp.float32
I32 = jnp.int32
BF16 = jnp.bfloat16

EA = 4
EB = 4
ES = 32
FAR_A = 8 * EA
FAR_B = 8 * EB
SLOTS_B = FAR_B + ES
M0 = 12
RUNGS = ((16, 12, 37), (18, 14, 42), (26, 20, 60))
ITERS = 8
STEP_W = 10.0
INVERSE = (0, 3, 4, 1, 2, 7, 8, 5, 6)
ORDER = (1, 2, 3, 4, 5, 6, 7, 8, 0)
BASE_A = tuple([None] + [(k - 1) * EA for k in range(1, 9)])
BASE = tuple([FAR_B] + [(k - 1) * EB for k in range(1, 9)])
CAP = tuple([ES] + [EB] * 8)
VMEM_LIMIT = 60 * 1024 * 1024
ANY = pl.BlockSpec(memory_space=pl.ANY)
SMEM = pl.BlockSpec(memory_space=pltpu.SMEM)
VMEM = pl.BlockSpec(memory_space=pltpu.VMEM)


def place():
    row, col = lax.axis_index("row"), lax.axis_index("col")
    return row, col


def at(row, col):
    return {"row": row, "col": col}


def flip_core(row):
    return row + 1 - 2 * lax.rem(row, 2)


def across(row):
    return lax.rem(row + ROWS // 2, ROWS)


def shift_x(row, step):
    within = lax.rem(row, 8)
    return row - within + lax.rem(within + 2 * step + 8, 8)


def neighbour(k, row, col):
    if k == 0:
        return at(flip_core(row), col)
    which, other = (k - 1) // 2, (k - 1) % 2
    if which < 2:
        row = shift_x(row, 1 if which == 0 else -1)
    else:
        col = lax.rem(col + (1 if which == 2 else COLS - 1), COLS)
    return at(flip_core(row) if other else row, col)


def greet(peers):
    barrier = pltpu.get_barrier_semaphore()
    for peer in peers:
        pl.semaphore_signal(barrier, inc=1, device_id=peer, device_id_type=MESH)
    pl.semaphore_wait(barrier, len(peers))


def send(src, dst, send_sem, recv_sem, peer):
    return pltpu.make_async_remote_copy(
        src_ref=src, dst_ref=dst, send_sem=send_sem, recv_sem=recv_sem, device_id=peer, device_id_type=MESH
    )


def first_kernel(
    spikes, stp, trace, held, pre, post, weights,
    tab, rtab, ptab, pidx, tables, rung, z0, early,
    pack, idx, mine, cnt, s1, r1, s2, r2, s3, r3, s4, r4, s5, r5, s6, r6,
):
    row, col = place()
    far = across(row)
    mate = at(far, col)
    barrier = pltpu.get_barrier_semaphore()

    @pl.loop(1, ROWS)
    def _(d):
        peer = at(lax.rem(row + d, ROWS), col)
        pl.semaphore_signal(barrier, inc=1, device_id=peer, device_id_type=MESH)

    for d in range(1, COLS):
        c = lax.rem(col + d, COLS)
        pl.semaphore_signal(barrier, inc=1, device_id=at(row, c), device_id_type=MESH)
        pl.semaphore_signal(barrier, inc=1, device_id=at(far, c), device_id_type=MESH)
    for k in (6, 8):
        pl.semaphore_signal(barrier, inc=1, device_id=neighbour(k, row, col), device_id_type=MESH)

    count_row = jnp.broadcast_to(held[...].astype(F32), (1, G))
    pack[pl.ds(0, STEPS), :] = spikes[...].astype(F32)
    pack[pl.ds(10, 2), :] = stp[...]
    pack[pl.ds(12, 3), :] = trace[...]
    pack[pl.ds(15, 1), :] = count_row
    mine[...] = count_row
    idx[...] = jnp.concatenate([pre[pl.ds(1, 1), :], post[pl.ds(1, 1), :], jnp.zeros((6, G), I32)], axis=0)
    cnt[col, row] = count_row
    tab[row] = pack[...]
    rtab[col] = pack[...]
    pl.semaphore_wait(barrier, ROWS - 1 + 2 * (COLS - 1) + 2)

    @pl.loop(1, ROWS)
    def _(d):
        peer = at(lax.rem(row + d, ROWS), col)
        send(mine, cnt.at[col, row], s5.at[d], r5.at[row], peer).start()

    @pl.loop(1, ROWS)
    def _(d):
        peer = at(lax.rem(row + d, ROWS), col)
        send(pack, tab.at[row], s1.at[d], r1.at[row], peer).start()

    small = []
    for d in range(1, COLS):
        c = lax.rem(col + d, COLS)
        small.append(send(pack, rtab.at[col], s2.at[d], r2.at[col], at(row, c)))
    for d in range(COLS):
        c = lax.rem(col + d, COLS)
        small.append(send(pack, ptab.at[col], s3.at[d], r3.at[col], at(far, c)))
    last = send(idx, pidx, s4.at[0], r4.at[0], mate)
    small.append(last)
    for copy in small:
        copy.start()
    ahead = [send(weights.at[pl.ds(HALF, M0)], z0, s6.at[0], r6.at[0], mate)]
    for k in range(1, 9):
        ahead.append(
            send(
                weights.at[pl.ds(HALF + M0 + BASE_A[k], EA)],
                early.at[pl.ds(BASE_A[INVERSE[k]], EA)],
                s6.at[k], r6.at[INVERSE[k]], neighbour(k, row, col),
            )
        )
    for copy in ahead[:5]:
        copy.start()

    @pl.loop(1, ROWS)
    def _(d):
        source = lax.rem(row + d, ROWS)
        send(mine, cnt.at[col, source], s5.at[d], r5.at[source], at(source, col)).wait()

    for d in range(1, COLS):
        c = lax.rem(col + d, COLS)
        send(cnt.at[col], cnt.at[col], s4.at[d], r4.at[1 + col], at(row, c)).start()
    for copy in ahead[5:]:
        copy.start()
    for d in range(1, COLS):
        c = lax.rem(col + d, COLS)
        send(cnt.at[c], cnt.at[c], s4.at[d], r4.at[1 + c], at(row, c)).wait()

    make_plan(row, col, cnt, tables, rung)

    @pl.loop(1, ROWS)
    def _(d):
        source = lax.rem(row + d, ROWS)
        send(pack, tab.at[source], s1.at[d], r1.at[source], at(source, col)).wait()

    for d in range(1, COLS):
        c = lax.rem(col + d, COLS)
        send(pack, rtab.at[c], s2.at[d], r2.at[c], at(row, c)).wait()
    for d in range(COLS):
        c = lax.rem(col + d, COLS)
        send(pack, ptab.at[c], s3.at[d], r3.at[c], at(far, c)).wait()
    last.wait()
    ahead[0].wait()
    for k in range(1, 9):
        send(
            weights.at[pl.ds(HALF + M0 + BASE_A[k], EA)], early.at[pl.ds(BASE_A[k], EA)], s6.at[k], r6.at[k],
            neighbour(k, row, col),
        ).wait()


def first(spikes, stp, trace, held, pre, post, weights):
    dma = pltpu.SemaphoreType.DMA
    return pl.pallas_call(
        first_kernel,
        out_shape=(
            jax.ShapeDtypeStruct((ROWS, 16, G), F32),
            jax.ShapeDtypeStruct((COLS, 16, G), F32),
            jax.ShapeDtypeStruct((COLS, 16, G), F32),
            jax.ShapeDtypeStruct((8, G), I32),
            jax.ShapeDtypeStruct((8, G), I32),
            jax.ShapeDtypeStruct((1,), I32),
            jax.ShapeDtypeStruct((M0, G, G), F32),
            jax.ShapeDtypeStruct((FAR_A, G, G), F32),
        ),
        in_specs=[VMEM] * 6 + [ANY],
        out_specs=(VMEM, VMEM, VMEM, VMEM, VMEM, SMEM, ANY, ANY),
        scratch_shapes=[
            pltpu.VMEM((16, G), F32), pltpu.VMEM((8, G), I32), pltpu.VMEM((1, G), F32),
            pltpu.VMEM((COLS, ROWS, 1, G), F32),
            dma((ROWS,)), dma((ROWS,)), dma((COLS,)), dma((COLS,)), dma((COLS,)), dma((COLS,)),
            dma((COLS,)), dma((COLS + 1,)), dma((ROWS,)), dma((ROWS,)), dma((9,)), dma((9,)),
        ],
        compiler_params=pltpu.CompilerParams(
            collective_id=0, has_side_effects=True, vmem_limit_bytes=VMEM_LIMIT
        ),
        name="first",
    )(spikes, stp, trace, held, pre, post, weights)


def make_plan(row, col, cnt, tables, rung):
    shape = (8, G)
    lane = lax.broadcasted_iota(I32, shape, 1)
    slot = lax.broadcasted_iota(I32, (1, G), 1)

    def pick(r, total):
        for c in range(COLS):
            total = jnp.where(slot == c * ROWS + r, cnt[c, r], total)
        return total

    total = lax.fori_loop(0, ROWS, pick, jnp.zeros((1, G), F32))
    count = jnp.broadcast_to(total, shape)
    surplus = jnp.maximum(count - HALF, 0.0)
    core = lax.rem(lane, 2)
    x_at = lax.rem(lane, 8) // 2
    z_hi = lax.rem(lane, 32) // 16

    def roll(value, by):
        return pltpu.roll(value, by % G, 1)

    def from_sibling(v):
        return jnp.where(core == 0, roll(v, -1), roll(v, 1))

    def seen(v):
        same = (
            jnp.where(x_at == 3, roll(v, 6), roll(v, -2)),
            jnp.where(x_at == 0, roll(v, -6), roll(v, 2)),
            roll(v, -ROWS),
            roll(v, ROWS),
        )
        out = [from_sibling(v)]
        for value in same:
            out += [value, from_sibling(value)]
        return out

    def toward(which, v):
        if which == 0:
            return jnp.where(x_at == 3, roll(v, 6), roll(v, -2))
        if which == 1:
            return jnp.where(x_at == 0, roll(v, -6), roll(v, 2))
        return roll(v, -ROWS if which == 2 else ROWS)

    def arriving(v):
        out = [from_sibling(v[0])]
        for k in range(1, 9):
            value = toward((k - 1) // 2, v[INVERSE[k]])
            out.append(from_sibling(value) if (k - 1) % 2 else value)
        return out

    def add(values):
        return functools.reduce(jnp.add, values)

    zero = jnp.zeros(shape, F32)
    free = jnp.maximum(surplus - M0, 0.0)
    top_a = [zero] + [jnp.clip(surplus - float(M0 + BASE_A[k]), 0.0, float(EA)) for k in range(1, 9)]
    top = [top_a[k] + float(CAP[k]) for k in range(9)]
    outs, ins = [zero] * 9, [zero] * 9
    for _ in range(ITERS):
        load = jnp.maximum(surplus - add(outs), float(M0)) + add(ins)
        near = seen(load)
        outs = [jnp.clip(outs[k] + (load - near[k]) * (1.0 / STEP_W), 0.0, top[k]) for k in range(9)]
        scale = jnp.minimum(1.0, free / jnp.maximum(add(outs), 1e-6))
        outs = [v * scale for v in outs]
        ins = arriving(outs)
    give = [jnp.minimum(jnp.floor(v + 0.5), top[k]) for k, v in enumerate(outs)]
    over = jnp.maximum(add(give) - free, 0.0)
    for k in range(9):
        less = jnp.minimum(give[k], over)
        give[k] = give[k] - less
        over = over - less
    give_a = [jnp.minimum(give[k], top_a[k]) for k in range(9)]
    give_b = [give[k] - give_a[k] for k in range(9)]
    take_a, take_b = arriving(give_a), arriving(give_b)
    rest = free - add(give)
    in_a, in_b = add(take_a), add(take_b[1:])
    later = in_b + take_b[0]
    picked = jnp.int32(len(RUNGS))
    m1 = jnp.int32(RUNGS[-1][0])
    most_a, most_b = jnp.max(in_a), jnp.max(in_b)
    for i in reversed(range(len(RUNGS))):
        a, b, size = RUNGS[i]
        need = jnp.max(a + later + jnp.maximum(rest - (a - in_a), 0.0))
        fits = (most_a <= float(a)) & (most_b <= float(b)) & (need <= float(size))
        picked = jnp.where(fits, i, picked)
        m1 = jnp.where(fits, a, m1)
    full = picked == len(RUNGS)
    rung[0] = picked

    me = col * ROWS + row
    mate = col * ROWS + across(row)

    def of(v, who):
        return jnp.max(jnp.where(lane == who, v, -1.0), axis=1, keepdims=True).astype(I32)[:1]

    def table(i, value, most):
        tables[pl.ds(i, 1), :] = jnp.clip(value, 0, most)

    none = jnp.zeros((1, 1), I32)
    held = of(count, me)
    a_me = [none] + [of(give_a[k], me) for k in range(1, 9)]
    left_me = [none] + [of(top_a[k] - give_a[k], me) for k in range(1, 9)]
    rest_me = of(rest, me)
    left_total = add(left_me)

    def nth(r):
        j = M0 + FAR_A + r - left_total
        before = none
        for k in range(1, 9):
            here = (r >= before) & (r < before + left_me[k])
            j = jnp.where(here, M0 + BASE_A[k] + a_me[k] + r - before, j)
            before = before + left_me[k]
        return j

    chosen = jnp.zeros((1, G), I32)
    before = rest_me
    for k in ORDER:
        here = (slot >= BASE[k]) & (slot < BASE[k] + CAP[k])
        chosen = jnp.where(here, slot - BASE[k] + before, chosen)
        before = before + of(give_b[k], me)
    table(0, nth(chosen), HALF - 1)
    in_a_me, later_me = of(in_a, me), of(later, me)
    early_own = jnp.minimum(rest_me, m1 - in_a_me)
    table(1, nth(jnp.where(slot < m1, slot - in_a_me, early_own + slot - m1 - later_me)), HALF - 1)
    source = jnp.zeros((1, G), I32)
    kind = jnp.zeros((1, G), I32)
    before = none
    for k in range(1, 9):
        amount = of(take_a[k], me)
        here = (slot >= before) & (slot < before + amount)
        source = jnp.where(here, BASE_A[k] + slot - before, source)
        kind = jnp.where(here, 1, kind)
        before = before + amount
    before = none + m1
    for k in ORDER:
        amount = of(take_b[k], me)
        here = (slot >= before) & (slot < before + amount)
        source = jnp.where(here, BASE[k] + slot - before, source)
        kind = jnp.where(here, 1, kind)
        before = before + amount
    table(2, source, SLOTS_B - 1)
    table(3, kind, 1)
    gather = jnp.zeros((1, G), I32)
    before = none
    for k in range(1, 9):
        here = (slot >= BASE_A[k]) & (slot < BASE_A[k] + EA)
        gather = jnp.where(here, slot - BASE_A[k] + before, gather)
        before = before + of(take_a[k], mate)
    before = none
    for k in ORDER:
        here = (slot >= FAR_A + BASE[k]) & (slot < FAR_A + BASE[k] + CAP[k])
        gather = jnp.where(here, slot - FAR_A - BASE[k] + before, gather)
        before = before + of(take_b[k], mate)
    table(4, gather, HALF - 1)
    j = slot - held
    in_a_mate, later_mate, rest_mate = of(in_a, mate), of(later, mate), of(rest, mate)
    early_mate = jnp.minimum(rest_mate, m1 - in_a_mate)
    total_left = none
    r = jnp.zeros((1, G), I32)
    by_a = jnp.zeros((1, G), I32)
    for k in range(1, 9):
        a_mate, left = of(give_a[k], mate), of(top_a[k] - give_a[k], mate)
        i = j - (M0 + BASE_A[k])
        here = (i >= 0) & (i < EA)
        by_a = jnp.where(here & (i < a_mate), 1, by_a)
        r = jnp.where(here, total_left + i - a_mate, r)
        total_left = total_left + left
    r = jnp.where(j >= M0 + FAR_A, total_left + j - (M0 + FAR_A), r)
    spot = jnp.where(r < early_mate, in_a_mate + r, m1 + later_mate + r - early_mate)
    before = rest_mate
    for k in ORDER:
        amount = of(give_b[k], mate)
        here = (r >= before) & (r < before + amount)
        spot = jnp.where(here, HALF + FAR_A + BASE[k] + r - before, spot)
        before = before + amount
    spot = jnp.where(by_a == 1, HALF + j - M0, spot)
    spot = jnp.where(full, j, spot)
    kind = jnp.where(j < 0, 0, jnp.where((j < M0) & jnp.logical_not(full), 2, 1))
    spot = jnp.where(kind == 2, j, spot)
    table(5, spot, HALF + FAR_A + SLOTS_B - 1)
    table(6, kind, 2)
    table(7, j, HALF - 1)


def move_kernel(
    sizes, tables, weights, early, staged,
    up, held_a, spread, imports, z1, z2, z3, got1, got2, got3, back, ls, ss, rs, zs, zr, gs, gr, as_, ar,
):
    m1, m2, size = sizes
    m3 = size - m1 - m2
    row, col = place()
    mate = at(across(row), col)
    peers = [neighbour(k, row, col) for k in range(9)]
    load = pltpu.make_async_copy(weights.at[pl.ds(HALF, HALF)], up, ls.at[0])
    load.start()
    load_a = pltpu.make_async_copy(early, held_a, ls.at[1])
    load_a.start()
    greet(peers + [mate])
    load_a.wait()
    load.wait()
    first_z = send(z1, got1, zs.at[0], zr.at[0], mate)
    second_z = send(z2, got2, zs.at[1], zr.at[1], mate)
    third_z = send(z3, got3, zs.at[2], zr.at[2], mate)

    @pl.loop(0, m1)
    def _(i):
        z1[i] = jnp.where(tables[3, i] == 1, held_a[jnp.minimum(tables[2, i], FAR_A - 1)], up[tables[1, i]])

    first_z.start()
    spreads = [
        send(spread.at[pl.ds(BASE[k], CAP[k])], imports.at[pl.ds(BASE[INVERSE[k]], CAP[k])], ss.at[k], rs.at[INVERSE[k]], peers[k])
        for k in range(9)
    ]
    for k in ORDER:

        @pl.loop(BASE[k], BASE[k] + CAP[k])
        def _(i):
            spread[i] = up[tables[0, i]]

        spreads[k].start()
    for k in range(9):
        send(spread.at[pl.ds(BASE[k], CAP[k])], imports.at[pl.ds(BASE[k], CAP[k])], ss.at[k], rs.at[k], peers[k]).wait_recv()

    def fill(target, start, count):
        @pl.loop(0, count)
        def _(i):
            t = start + i
            target[i] = jnp.where(tables[3, t] == 1, imports[tables[2, t]], up[tables[1, t]])

    fill(z2, m1, m2)
    second_z.start()
    fill(z3, m1 + m2, m3)
    third_z.start()

    def onward(k, part):
        if part == 0:
            base, there, n, s, r = BASE_A[k], BASE_A[INVERSE[k]], EA, as_, ar
        else:
            base, there, n, s, r = FAR_A + BASE[k], FAR_A + BASE[INVERSE[k]], CAP[k], gs, gr
        go = send(back.at[pl.ds(base, n)], staged.at[pl.ds(HALF + there, n)], s.at[k], r.at[INVERSE[k]], peers[k])
        come = send(back.at[pl.ds(base, n)], staged.at[pl.ds(HALF + base, n)], s.at[k], r.at[k], peers[k])
        return base, n, go, come

    waits = []
    first_z.wait_recv()
    for k in range(1, 9):
        base, n, go, come = onward(k, 0)

        @pl.loop(base, base + n)
        def _(i):
            back[i] = got1[jnp.minimum(tables[4, i], m1 - 1)]

        go.start()
        waits.append(come)
    out1 = pltpu.make_async_copy(got1, staged.at[pl.ds(0, m1)], ls.at[1])
    out1.start()
    second_z.wait_recv()
    for k in range(1, 9):
        base, n, go, come = onward(k, 1)

        @pl.loop(base, base + n)
        def _(i):
            back[i] = got2[jnp.minimum(tables[4, i], m2 - 1)]

        go.start()
        waits.append(come)
    out2 = pltpu.make_async_copy(got2, staged.at[pl.ds(m1, m2)], ls.at[2])
    out2.start()
    third_z.wait_recv()
    out3 = pltpu.make_async_copy(got3, staged.at[pl.ds(m1 + m2, m3)], ls.at[3])
    out3.start()
    base, n, go, come = onward(0, 1)

    @pl.loop(base, base + n)
    def _(i):
        t = tables[4, i]
        back[i] = jnp.where(t < m2, got2[jnp.minimum(t, m2 - 1)], got3[jnp.clip(t - m2, 0, m3 - 1)])

    go.start()
    waits.append(come)
    out1.wait()
    out2.wait()
    out3.wait()
    first_z.wait_send()
    second_z.wait_send()
    third_z.wait_send()
    for k in range(9):
        spreads[k].wait_send()
    for come in waits:
        come.wait()


def full_kernel(weights, staged, ss, rs):
    row, col = place()
    mate = at(across(row), col)
    greet([mate])
    copy = send(weights.at[pl.ds(HALF, HALF)], staged.at[pl.ds(0, HALF)], ss, rs, mate)
    copy.start()
    copy.wait()


STAGED = jax.ShapeDtypeStruct((HALF + FAR_A + SLOTS_B, G, G), F32)


def move(index, tables, weights, early):
    dma = pltpu.SemaphoreType.DMA
    if index == len(RUNGS):
        return pl.pallas_call(
            full_kernel,
            out_shape=STAGED,
            in_specs=[ANY],
            out_specs=ANY,
            scratch_shapes=[dma, dma],
            compiler_params=pltpu.CompilerParams(
                collective_id=2 + index, has_side_effects=True, vmem_limit_bytes=VMEM_LIMIT
            ),
            name="move_full",
        )(weights)
    m1, m2, size = RUNGS[index]
    m3 = size - m1 - m2

    def blocks(n):
        return pltpu.VMEM((n, G, G), F32)

    return pl.pallas_call(
        functools.partial(move_kernel, RUNGS[index]),
        out_shape=STAGED,
        in_specs=[SMEM, ANY, ANY],
        out_specs=ANY,
        scratch_shapes=[
            blocks(HALF), blocks(FAR_A), blocks(SLOTS_B), blocks(SLOTS_B), blocks(m1), blocks(m2), blocks(m3),
            blocks(m1), blocks(m2), blocks(m3), blocks(FAR_A + SLOTS_B),
            dma((4,)), dma((9,)), dma((9,)), dma((3,)), dma((3,)), dma((9,)), dma((9,)), dma((9,)), dma((9,)),
        ],
        compiler_params=pltpu.CompilerParams(
            collective_id=2 + index, has_side_effects=True, vmem_limit_bytes=VMEM_LIMIT
        ),
        name=f"move_{size}",
    )(tables, weights, early)


CHUNK = 8
KP = 64


def split(value):
    high = value.astype(BF16)
    return high, (value - high.astype(F32)).astype(BF16)


def blocks_kernel(
    tables, pre, post, pidx, tab, rtab, ptab, weights, staged, z0, new, cur, qs, ds, ps, scr, acc, win, wout, sem_in, sem_out
):
    steps = HALF // CHUNK

    def fetch(step, slot):
        for b in range(CHUNK):
            s = step * CHUNK + b
            moved = tables[6, s]

            @pl.when(moved == 0)
            def _():
                pltpu.make_async_copy(weights.at[s], win.at[slot, b], sem_in.at[slot]).start()

            @pl.when(moved == 1)
            def _():
                pltpu.make_async_copy(staged.at[tables[5, s]], win.at[slot, b], sem_in.at[slot]).start()

            @pl.when(moved == 2)
            def _():
                pltpu.make_async_copy(z0.at[jnp.minimum(tables[5, s], M0 - 1)], win.at[slot, b], sem_in.at[slot]).start()

    fetch(0, 0)
    fetch(1, 1)
    neuron = lax.broadcasted_iota(I32, (1, G), 1)
    lane = lax.broadcasted_iota(I32, (G, G), 1)
    polarity = jnp.where(lax.rem(neuron, 5) == 4, -INHIB_GAIN, 1.0).astype(F32)

    use, supply, fast = tab[:, 10, :], tab[:, 11, :], tab[:, 12, :]
    scr[...] = jnp.zeros_like(scr)
    for t in range(STEPS):
        s = tab[:, t, :]
        use = BASE_USE + (use - BASE_USE) * USE_DECAY
        use = use + s * BASE_USE * (1.0 - use)
        release = s * use * supply
        supply = supply + SUPPLY_RATE * (1.0 - supply) - release
        fast = fast * PLUS_DECAY + s
        scr[:, t, :] = fast
        scr[:, STEPS + t, :] = release

    @pl.loop(0, ROWS, unroll=8)
    def _(g):
        terms = scr[g]
        high = terms.astype(BF16).astype(F32)
        low = terms - high
        qs[g] = jnp.concatenate([high[:20], low[:20], high[:20], jnp.zeros((4, G), F32)], axis=0).astype(BF16)
        driven = terms[STEPS : 2 * STEPS] * polarity
        dh = driven.astype(BF16).astype(F32)
        dl = driven - dh
        pad6 = jnp.zeros((6, G), F32)
        wide = jnp.concatenate([dh, pad6, dl, pad6, jnp.zeros((G - 32, G), F32)], axis=0)
        tall = jnp.transpose(wide)
        only = jnp.where(lane < 16, tall, 0.0)
        ds[g, pl.ds(0, G), :] = tall.astype(BF16)
        ds[g, pl.ds(G, G), :] = only.astype(BF16)

    for half, source in enumerate((rtab, ptab)):
        fast_p, slow_p = source[:, 13, :], source[:, 14, :]
        for t in range(STEPS):
            s = source[:, t, :]
            scr[pl.ds(half * COLS, COLS), t, :] = s * (PAIR_UP + TRIPLET_UP * slow_p)
            scr[pl.ds(half * COLS, COLS), STEPS + t, :] = -(PAIR_DOWN * fast_p)
            fast_p = fast_p * MINUS_DECAY + s
            slow_p = slow_p * SLOW_DECAY + s

    @pl.loop(0, 2 * COLS, unroll=8)
    def _(g):
        terms = scr[g] * LEARN_RATE
        high = terms.astype(BF16).astype(F32)
        low = terms - high
        rows = jnp.concatenate([high[:20], high[:20], low[:20], jnp.zeros((G - 60, G), F32)], axis=0)
        ps[g] = jnp.transpose(rows).astype(BF16)

    acc[...] = jnp.zeros_like(acc)

    @pl.loop(0, steps)
    def _(step):
        slot = lax.rem(step, 3)
        pltpu.make_async_copy(weights.at[pl.ds(0, CHUNK)], win.at[slot], sem_in.at[slot]).wait()

        @pl.when(step + 2 < steps)
        def _():
            fetch(step + 2, lax.rem(step + 2, 3))

        @pl.when(step >= 2)
        def _():
            pltpu.make_async_copy(wout.at[0], new.at[pl.ds(0, CHUNK)], sem_out.at[lax.rem(step, 2)]).wait()

        o = lax.rem(step, 2)
        currents = []
        for b in range(CHUNK):
            s = step * CHUNK + b
            moved, there = tables[6, s] >= 1, tables[7, s]
            p = jnp.where(moved, pidx[0, there], pre[s])
            q = jnp.where(moved, pidx[1, there] + COLS, post[s])
            w = win[slot, b]
            change = jnp.dot(ps[q][:, :KP], qs[p], preferred_element_type=F32)
            wh, wl = split(w)
            currents.append((q, jnp.dot(jnp.concatenate([wh, wl], axis=1), ds[p], preferred_element_type=F32)))
            wout[o, b] = jnp.clip(w + change, 0.0, WEIGHT_MAX)
        for q, value in currents:
            acc[q] += value
        pltpu.make_async_copy(wout.at[o], new.at[pl.ds(step * CHUNK, CHUNK)], sem_out.at[o]).start()

    for q in range(2 * COLS):
        turned = jnp.transpose(acc[q])
        cur[q] = turned[0:16] + turned[16:32]
    for o in range(2):
        pltpu.make_async_copy(wout.at[o], new.at[pl.ds(0, CHUNK)], sem_out.at[o]).wait()


def do_blocks(tables, pre, post, pidx, tab, rtab, ptab, weights, staged, z0):
    dma = pltpu.SemaphoreType.DMA
    return pl.pallas_call(
        blocks_kernel,
        out_shape=(jax.ShapeDtypeStruct((HALF, G, G), F32), jax.ShapeDtypeStruct((2 * COLS, 16, G), F32)),
        in_specs=[SMEM, SMEM, SMEM, SMEM, VMEM, VMEM, VMEM, ANY, ANY, ANY],
        out_specs=(ANY, VMEM),
        scratch_shapes=[
            pltpu.VMEM((ROWS, KP, G), BF16),
            pltpu.VMEM((ROWS, 2 * G, G), BF16),
            pltpu.VMEM((2 * COLS, G, G), BF16),
            pltpu.VMEM((ROWS, 24, G), F32),
            pltpu.VMEM((2 * COLS, G, G), F32),
            pltpu.VMEM((3, CHUNK, G, G), F32),
            pltpu.VMEM((2, CHUNK, G, G), F32),
            dma((3,)), dma((2,)),
        ],
        compiler_params=pltpu.CompilerParams(vmem_limit_bytes=VMEM_LIMIT),
        name="blocks",
    )(tables, pre, post, pidx, tab, rtab, ptab, weights, staged, z0)


def currents_kernel(cur, out, got, ss, rs):
    row, col = place()
    far = across(row)
    peers, copies, arrivals = [], [], []
    for d in range(1, COLS):
        c = lax.rem(col + d, COLS)
        peers.append(at(row, c))
        copies.append(send(cur.at[c], got.at[col], ss.at[d], rs.at[col], at(row, c)))
        arrivals.append(send(cur.at[c], got.at[c], ss.at[d], rs.at[c], at(row, c)))
    for d in range(COLS):
        c = lax.rem(col + d, COLS)
        peers.append(at(far, c))
        copies.append(send(cur.at[COLS + c], got.at[COLS + col], ss.at[COLS + d], rs.at[COLS + col], at(far, c)))
        arrivals.append(send(cur.at[COLS + c], got.at[COLS + c], ss.at[COLS + d], rs.at[COLS + c], at(far, c)))
    greet(peers)
    for copy in copies:
        copy.start()
    got[col] = cur[col]
    for copy in arrivals:
        copy.wait()
    drive = got[0]
    for i in range(1, 2 * COLS):
        drive = drive + got[i]
    gain = 1.0 / math.sqrt(G * HALF)
    state = jnp.zeros((1, G), F32)
    for t in range(STEPS):
        state = state * SYN_DECAY + gain * drive[t : t + 1]
        out[pl.ds(t, 1), :] = state


def settle(cur):
    dma = pltpu.SemaphoreType.DMA
    return pl.pallas_call(
        currents_kernel,
        out_shape=jax.ShapeDtypeStruct((STEPS, G), F32),
        in_specs=[VMEM],
        out_specs=VMEM,
        scratch_shapes=[pltpu.VMEM((2 * COLS, 16, G), F32), dma((2 * COLS,)), dma((2 * COLS,))],
        compiler_params=pltpu.CompilerParams(collective_id=1, has_side_effects=True),
        name="currents",
    )(cur)


def body(spikes, stp_init, trace_init, weights, block_pre, block_post, block_count):
    own = weights[0, 0]
    pre, post = block_pre[0, 0], block_post[0, 0]
    tab, rtab, ptab, pidx, tables, rung, z0, early = first(
        spikes, stp_init, trace_init, block_count, pre.reshape(2, G), post.reshape(2, G), own
    )
    staged = lax.switch(
        rung[0], [functools.partial(move, i) for i in range(len(RUNGS) + 1)], tables, own, early
    )
    new, cur = do_blocks(tables, pre, post, pidx, tab, rtab, ptab, own, staged, z0)
    synaptic = settle(cur)
    return (new[None, None], synaptic)


def solution(mesh):
    placed = (
        P(None, ("row", "col")),
        P(None, ("row", "col")),
        P(None, ("row", "col")),
        P("row", "col", None, None, None),
        P("row", "col", None),
        P("row", "col", None),
        P("row", "col"),
    )
    return jax.shard_map(
        body,
        mesh=mesh,
        in_specs=placed,
        out_specs=(P("row", "col", None, None, None), P(None, ("row", "col"))),
        check_vma=False,
    )
```

time: 241 us -> 132 us (0.55)
  Pallas kernels: 233 us -> 128 us
  other arithmetic: 2.72 us -> 0 us
    pallas_call x3 -> x2, Pallas kernels: 207 us -> 104 us  [the longest x1 71 us: move(): pl.pallas_call(functools.partial(move_kernel, RUNGS[index]), out_shape=ST...]
    pallas_call x1, Pallas kernels: 16.2 us -> 12.8 us  [do_blocks(): pl.pallas_call(blocks_kernel, out_shape=(jax.ShapeDtypeStruct((HALF, G, G...]
where the time goes in v2:
time: 132 us; the launch traced here: 131 us
  Pallas kernels  128 us (97%)
  between operations  1.93 us (1%)
    pallas_call x1, Pallas kernels, move(): pl.pallas_call(functools.partial(move_kernel, RUNGS[index]), out_shape=ST...  71 us
    pallas_call x1, Pallas kernels, first(): pl.pallas_call(first_kernel, out_shape=(jax.ShapeDtypeStruct((ROWS, 16, G...  33.4 us
    pallas_call x1, Pallas kernels, do_blocks(): pl.pallas_call(blocks_kernel, out_shape=(jax.ShapeDtypeStruct((HALF, G, G...  12.8 us
    pallas_call x1, Pallas kernels, settle(): pl.pallas_call(currents_kernel, out_shape=jax.ShapeDtypeStruct((STEPS, G)...  10.4 us

profile of v2, /device:TPU:0, one launch (start us, length us, event | category | flops | bytes accessed | tf_op | source)
XLA Modules:
  0.0 130.8 jit_solution(17403451309590575967)
XLA Ops:
  1.3 33.4 %first.1 = (f32[32,16,128]{2,1,0:T(8,128)}, f32[4,16,128]{2,1,0:T(8,128)}, f32[4,16,128]{2,1,0:T(8,128)}, s32[8,128]{1,0:T(8,128)}, s32[8,128]{1,0:T(8,128)S(1)}...) custom-call(s32[10,128]{1,0:T(8,128)} %spikes.1, f32[2,128]{1,0:T(2,128)} %stp.1, ...), custom_call_target="tpu_custom_call" | custom-call | tf_op jit(solution)/shard_map/first/pallas_call | solution.py:207
  35.3 71.0 %conditional.1 = (f32[224,128,128]{2,1,0:T(8,128)}) conditional(s32[]{:T(128)} %bitcast.5, (s32[8,128]{1,0:T(8,128)S(1)}, f32[256,128,128]{2,1,0:T(8,128)}, f32[32,128,128]{2,1,0:T(8,128)S(1)}) %tuple.28, (s32[8,128]{1,0:T(8,128)S(1)}, f32[256,128,128]{2,1,0:T(8,128)}, f32[32,128,128]{2,1,0:T(8,128)S(1)}) %tuple.29, ...), branch_computations={%region_0.0_spmd, %region_1.0_spmd, %region_2.0_spmd, %region_3.0_... | conditional | bytes 8 | solution.py:765
  35.3 71.0 %move_42.1 = f32[224,128,128]{2,1,0:T(8,128)} custom-call(s32[8,128]{1,0:T(8,128)S(1)} %get-tuple-element.27.tables, f32[256,128,128]{2,1,0:T(8,128)} %get-tuple-element.28.weights, f32[32,128,128]{2,1,0:T(8,128)S(1)} %get-tuple-element.29.early), custom_call_target="tpu_custom_call" | custom-call | tf_op jit(solution)/shard_map/cond/branch_1_fun/move_42/pallas_call | solution.py:557
  106.3 12.8 %blocks.1 = (f32[128,128,128]{2,1,0:T(8,128)}, f32[8,16,128]{2,1,0:T(8,128)}) custom-call(s32[8,128]{1,0:T(8,128)S(1)} %get-tuple-element.45.tables, s32[256]{0:T(256)} %bitcast.14, s32[256]{0:T(256)} %bitcast.16, s32[8,128]{1,0:T(8,128)} %get-tuple-element.46.pidx, f32[32,16,128]{2,1,0:T(8,128)} %get-tuple-element.47.tab, ...), custom_call_target="tpu_custom_call" | custom-call | tf_op jit(solution)/shard_map/blocks/pallas_call | solution.py:696
  119.1 10.4 %currents.1 = f32[10,128]{1,0:T(8,128)} custom-call(f32[8,16,128]{2,1,0:T(8,128)} %get-tuple-element.54.cur), custom_call_target="tpu_custom_call" | custom-call | tf_op jit(solution)/shard_map/currents/pallas_call | solution.py:748
  129.5 1.3 copy.15
